TPU v7x, 16 devices: a 4x2x1 block of a 4x4x8 slice. The times are simulated.
16 devices in a mesh: dp: 2 (over y, z), tp: 8 (over x, core).
Axes of the slice: x: 4, y: 2, z: 1, core: 2. Of those that a mesh axis runs over, the one named last changes fastest.
The devices are a block of a 4x4x8 slice.
Arguments:
- X: bfloat16 [512, 4096], P(('dp', 'tp')), parts along dimension 0
- dY: bfloat16 [512, 4096], P(('dp', 'tp')), parts along dimension 0
- W1: bfloat16 [4096, 14336], P(None, 'tp')
- W2: bfloat16 [14336, 4096], P('tp')
Outputs:
- output 1: bfloat16 [512, 4096], P(('dp', 'tp')), parts along dimension 0
- output 2: float32 [8192, 14336], P('dp', 'tp'), parts along dimension 0
- output 3: float32 [28672, 4096], P(('dp', 'tp')), parts along dimension 0
There are 2 independent parts. A program takes and returns all parts, laid end to end along the dimension named above; an argument that names none is the same for every part.
All inputs are finite; a program needn't handle non-finite values.
Results may differ from a plain program's by a relative error of at most 0.00941025.
Values are sent between devices in bfloat16 or wider.
A program may use at most 768 MiB of HBM per device.

v0:
```python
import functools
import math

import jax
import jax.numpy as jnp
from jax import lax
from jax.experimental import pallas as pl
from jax.experimental.pallas import tpu as pltpu
from jax.sharding import PartitionSpec as P

C0 = math.sqrt(2.0 / math.pi)
C1 = 0.044715
F32 = jnp.float32
BF16 = jnp.bfloat16
NP = 4
NW = 16
TILE = 896
XC = (2, 2, 2, 2)
YC = (2, 2, 2, 1, 1)
LEAD = 3
LA = 2
AR = 3
GIVE = 1
VMEM_LIMIT = 62 * 2 ** 20
NT = (((1,), (1,)), ((), ()))
TN = (((0,), (0,)), ((), ()))


def _gelu(u):
    u2 = u * u
    t = jnp.tanh(u * (C0 + (C0 * C1) * u2))
    p = 0.5 + 0.5 * t
    return u * p, p + (u * (1.0 - t * t)) * (0.5 * C0 + (1.5 * C0 * C1) * u2)


def _forward_kernel(ntp, x, dy, w1, w2, xg_o, dyg_o, z_o, dz_o, r_o,
                    xg, dyg, w1v, w2v, w1p, acc, dact, z, dz, dzp, part, rr,
                    lsem, wsem, osem, ssem, rsem, xsem, psem):
    nchip = ntp // 2
    rows, h = x.shape
    half = h // 2
    hp = half // NP
    hw = half // NW
    f = w1.shape[1]
    me = lax.axis_index('tp')
    c = lax.rem(me, 2)
    chip = me // 2
    partner = me + 1 - 2 * c
    right = lax.rem(chip + 1, nchip) * 2 + c
    left = lax.rem(chip + nchip - 1, nchip) * 2 + c
    opp = lax.rem(chip + 2, nchip) * 2 + c
    fsrc = left * (1 - c) + right * c
    fdst = right * (1 - c) + left * c
    flip = 1 - 2 * c
    chunks = []
    for src, buf, sizes in ((x, xg, XC), (dy, dyg, YC)):
        for k, n in enumerate(sizes):
            chunks.append((src, buf, pl.ds(sum(sizes[:k]) * (h // 8), n * (h // 8))))
    nx, nq = len(XC), len(chunks)

    def piece(q, dev):
        _, buf, cols = chunks[q]
        return buf.at[pl.ds(pl.multiple_of(dev * rows, rows), rows), cols]

    def rcopy(q, slot, dev, to):
        return pltpu.make_async_remote_copy(
            src_ref=piece(q, dev), dst_ref=piece(q, dev), send_sem=ssem.at[q, slot], recv_sem=rsem.at[q, slot],
            device_id={'tp': to}, device_id_type=pl.DeviceIdType.MESH)

    own, wcp = [], []
    for q, (src, buf, cols) in enumerate(chunks):
        cp = pltpu.make_async_copy(src.at[:, cols], piece(q, me), lsem.at[q])
        cp.start()
        own.append(cp)
    for q, (src, buf, cols) in enumerate(chunks):
        wr, wb = (w1.at[cols, :], w1v.at[cols, :]) if q < nx else (w2.at[:, cols], w2v.at[:, cols])
        cp = pltpu.make_async_copy(wr, wb, wsem.at[q])
        cp.start()
        wcp.append(cp)

    barrier = pltpu.get_barrier_semaphore()
    for nb in (partner, right, left):
        pl.semaphore_signal(barrier, inc=1, device_id={'tp': nb}, device_id_type=pl.DeviceIdType.MESH)
    pl.semaphore_wait(barrier, 3)

    started = []

    def send(q, slot, dev, to):
        cp = rcopy(q, slot, dev, to)
        cp.start()
        started.append(cp)

    def send_own(q):
        own[q].wait()
        send(q, 0, me, right)
        send(q, 1, me, left)
        send(q, 3, me, partner)

    def hop(q):
        rcopy(q, 0, left, me + 0).wait_recv()
        rcopy(q, 1, right, me + 0).wait_recv()
        send(q, 2, fsrc, fdst)
        send(q, 4, left, partner)
        send(q, 5, right, partner)

    def last(q):
        rcopy(q, 2, opp, me + 0).wait_recv()
        send(q, 6, opp, partner)

    def arrived(q):
        rcopy(q, 3, partner, me + 0).wait_recv()
        rcopy(q, 4, left + flip, me + 0).wait_recv()
        rcopy(q, 5, right + flip, me + 0).wait_recv()
        rcopy(q, 6, opp + flip, me + 0).wait_recv()

    outs = []

    def put(src, dst):
        cp = pltpu.make_async_copy(src, dst, osem.at[len(outs)])
        cp.start()
        outs.append(cp)

    def weights(i):
        src = pl.ds(pl.multiple_of((1 - c) * half + i * hw, hw), hw)
        return pltpu.make_async_remote_copy(
            src_ref=w1v.at[src, :], dst_ref=w1p.at[pl.ds(i * hw, hw), :],
            send_sem=xsem.at[0, i], recv_sem=xsem.at[1, i],
            device_id={'tp': partner}, device_id_type=pl.DeviceIdType.MESH)

    tiles = [(lo, min(TILE, f - lo)) for lo in range(0, f, TILE)]

    def swap(i):
        cols = pl.ds(*tiles[i])
        return pltpu.make_async_remote_copy(
            src_ref=dz.at[:, cols], dst_ref=dzp.at[:, cols], send_sem=psem.at[0, i], recv_sem=psem.at[1, i],
            device_id={'tp': partner}, device_id_type=pl.DeviceIdType.MESH)

    def begin(cp):
        cp.start()
        started.append(cp)

    def compute(q):
        _, buf, hcols = chunks[q]
        if q >= nx:
            wcp[q].wait()
        ends = q in (nx - 1, nq - 1)
        for i, (lo, wide) in enumerate(tiles if ends else [(0, f)]):
            cols = pl.ds(lo, wide)
            if q < nx:
                p = jnp.dot(buf[:, hcols], w1v[hcols, cols], preferred_element_type=F32)
            else:
                p = lax.dot_general(buf[:, hcols], w2v[cols, hcols], NT, preferred_element_type=F32)
            if q not in (0, nx):
                p += acc[:, cols]
            if q == nx - 1:
                g0, g1 = _gelu(p.astype(BF16).astype(F32))
                z[:, cols] = g0.astype(BF16)
                dact[:, cols] = g1
            elif q == nq - 1:
                dz[:, cols] = (p * dact[:, cols]).astype(BF16)
                begin(swap(i))
            else:
                acc[:, cols] = p
        if q == nx - 1:
            put(xg, xg_o)
            put(z, z_o)
        elif q == nq - 1:
            put(dyg, dyg_o)

    def use(q):
        arrived(q)
        compute(q)

    for q in range(min(LEAD, nq)):
        send_own(q)
    given = 0
    for s in range(nq + AR):
        if s < nq:
            hop(s)
            if s + LEAD < nq:
                send_own(s + LEAD)
        if 0 <= s - LA < nq:
            last(s - LA)
        if s == GIVE:
            for q in range(nx):
                wcp[q].wait()
        if GIVE <= s < nq:
            for i in range(given, NW * (s - GIVE + 1) // (nq - GIVE)):
                begin(weights(i))
                given += 1
        if 0 <= s - AR < nq:
            use(s - AR)

    put(dz, dz_o)
    for j in range(NP):
        rws = pl.ds(pl.multiple_of(c * half + j * hp, hp), hp)
        part[j] = lax.dot_general(dz[...], w1v[rws, :], NT, preferred_element_type=F32)
    for i in range(NW):
        weights(i).wait_recv()
    for i in range(len(tiles)):
        swap(i).wait_recv()
    for j in range(NP):
        p = lax.dot_general(dzp[...], w1p[pl.ds(j * hp, hp), :], NT, preferred_element_type=F32)
        cols = pl.ds(j * hp, hp)
        rr[:, cols] = (part[j] + p).astype(BF16)
        put(rr.at[:, cols], r_o.at[:, cols])
    for cp in started:
        cp.wait_send()
    for cp in outs:
        cp.wait()


def _weight_grad_kernel(xg, dyg, z, dz, dw1, dw2, xa, dya, za, dza, b1, b2, isem, sem1, sem2):
    t, h = xg.shape
    nq = 4
    hc = h // nq
    f = z.shape[1]
    n1, n2 = b1.shape[0], b2.shape[0]
    t1, t2 = b1.shape[1], b2.shape[1]
    k1, k2 = h // t1, f // t2
    cz = pltpu.make_async_copy(z, za, isem.at[0])
    cy = [pltpu.make_async_copy(dyg.at[:, pl.ds(q * hc, hc)], dya.at[:, pl.ds(q * hc, hc)], isem.at[1 + q]) for q in range(nq)]
    cx = pltpu.make_async_copy(xg, xa, isem.at[1 + nq])
    cd = pltpu.make_async_copy(dz, dza, isem.at[2 + nq])
    for cp in [cz] + cy + [cd, cx]:
        cp.start()
    cz.wait()

    def out2(i):
        s = lax.rem(i, n2)
        return pltpu.make_async_copy(b2.at[s], dw2.at[pl.ds(pl.multiple_of(i * t2, t2), t2), :], sem2.at[s])

    def out1(i):
        s = lax.rem(i, n1)
        return pltpu.make_async_copy(b1.at[s], dw1.at[pl.ds(pl.multiple_of(i * t1, t1), t1), :], sem1.at[s])

    for q in range(nq):
        cy[q].wait()
        b2[0, :, pl.ds(q * hc, hc)] = lax.dot_general(za[:, :t2], dya[:, pl.ds(q * hc, hc)], TN, preferred_element_type=F32)
    out2(0).start()

    @pl.loop(1, k2)
    def _(i):
        @pl.when(i >= n2)
        def _():
            out2(i - n2).wait()
        zt = za[:, pl.ds(pl.multiple_of(i * t2, t2), t2)]
        s = lax.rem(i, n2)
        for q in range(nq):
            b2[s, :, pl.ds(q * hc, hc)] = lax.dot_general(zt, dya[:, pl.ds(q * hc, hc)], TN, preferred_element_type=F32)
        out2(i).start()

    cx.wait()
    cd.wait()

    @pl.loop(0, k1)
    def _(i):
        @pl.when(i >= n1)
        def _():
            out1(i - n1).wait()
        xt = xa[:, pl.ds(pl.multiple_of(i * t1, t1), t1)]
        b1[lax.rem(i, n1)] = lax.dot_general(xt, dza[...], TN, preferred_element_type=F32)
        out1(i).start()

    for i in range(max(0, k2 - n2), k2):
        out2(i).wait()
    for i in range(max(0, k1 - n1), k1):
        out1(i).wait()


def solution(mesh):
    ntp = mesh.shape['tp']
    nchip = ntp // 2
    any_spec = pl.BlockSpec(memory_space=pl.ANY)

    def body(x, dy, w1, w2):
        rows, h = x.shape
        f = w1.shape[1]
        t, half = rows * ntp, h // 2
        nt = -(-f // TILE)
        nq = len(XC) + len(YC)
        sds = jax.ShapeDtypeStruct
        dma = pltpu.SemaphoreType.DMA
        xg, dyg, z, dz, r = pl.pallas_call(
            functools.partial(_forward_kernel, ntp),
            name='gather_forward',
            out_shape=[sds((t, h), BF16), sds((t, h), BF16), sds((t, f), BF16), sds((t, f), BF16),
                       sds((t, half), BF16)],
            in_specs=[any_spec] * 4,
            out_specs=[any_spec] * 5,
            scratch_shapes=[
                pltpu.VMEM((t, h), BF16),
                pltpu.VMEM((t, h), BF16),
                pltpu.VMEM((h, f), BF16),
                pltpu.VMEM((f, h), BF16),
                pltpu.VMEM((half, f), BF16),
                pltpu.VMEM((t, f), F32),
                pltpu.VMEM((t, f), F32),
                pltpu.VMEM((t, f), BF16),
                pltpu.VMEM((t, f), BF16),
                pltpu.VMEM((t, f), BF16),
                pltpu.VMEM((NP, t, half // NP), F32),
                pltpu.VMEM((t, half), BF16),
                dma((nq,)), dma((nq,)), dma((4 + NP,)),
                dma((nq, 7)), dma((nq, 7)), dma((2, NW)), dma((2, nt)),
            ],
            compiler_params=pltpu.CompilerParams(
                collective_id=0, has_side_effects=True, vmem_limit_bytes=VMEM_LIMIT),
            cost_estimate=pl.CostEstimate(flops=6 * t * h * f, bytes_accessed=4 * h * f, transcendentals=t * f),
        )(x, dy, w1, w2)

        r = lax.all_to_all(r.reshape(ntp, rows, half), 'tp', 0, 0, tiled=True)
        t1, t2 = 512, 256
        dw1, dw2 = pl.pallas_call(
            _weight_grad_kernel,
            name='weight_grads',
            out_shape=[sds((h, f), F32), sds((f, h), F32)],
            in_specs=[any_spec] * 4,
            out_specs=[any_spec] * 2,
            scratch_shapes=[
                pltpu.VMEM((t, h), BF16),
                pltpu.VMEM((t, h), BF16),
                pltpu.VMEM((t, f), BF16),
                pltpu.VMEM((t, f), BF16),
                pltpu.VMEM((4, t1, f), F32),
                pltpu.VMEM((4, t2, h), F32),
                dma((7,)), dma((4,)), dma((4,)),
            ],
            compiler_params=pltpu.CompilerParams(vmem_limit_bytes=VMEM_LIMIT),
            cost_estimate=pl.CostEstimate(flops=4 * t * h * f, bytes_accessed=8 * h * f, transcendentals=0),
        )(xg, dyg, z, dz)
        r = r.astype(F32)
        dx = jnp.concatenate([sum(r[2 * i + k] for i in range(nchip)) for k in range(2)], axis=1).astype(BF16)
        return dx, dw1, dw2

    return jax.shard_map(
        body, mesh=mesh,
        in_specs=(P(('dp', 'tp'), None), P(('dp', 'tp'), None), P(None, 'tp'), P('tp', None)),
        out_specs=(P(('dp', 'tp'), None), P('dp', 'tp'), P(('dp', 'tp'), None)),
        check_vma=False)
```

profile of v0, /device:TPU:113, one launch (start us, length us, event | category | flops | bytes accessed | tf_op | source)
XLA Modules:
  0.0 62.0 jit_solution(5801595091292420686)
XLA Ops:
  0.6 35.3 %gather_forward.1 = (bf16[256,4096]{1,0:T(8,128)(2,1)}, bf16[256,4096]{1,0:T(8,128)(2,1)}, bf16[256,1792]{1,0:T(8,128)(2,1)}, bf16[256,1792]{1,0:T(8,128)(2,1)}, bf16[256,2048]{1,0:T(8,128)(2,1)}) custom-call(bf16[32,4096]{1,0:T(8,128)(2,1)} %x.1, bf16[32,4096]{1,0:T(8,128)(2,1)} %dy.1, bf16[4096,1792]{1,0:T(8,128)(2,1)} %w1.1, bf16[1792,4096]{1,0:T(8,128)(2,1)} %w2.1), custom_call_target="tpu_custom_call" | custom-call | flops 11274289152 | bytes 29360128 | tf_op jit(solution)/shard_map/gather_forward/pallas_call | solution.py:284
  35.9 3.7 %all-to-all-start = ((bf16[8,32,2048]{2,1,0:T(8,128)(2,1)}), bf16[8,32,2048]{2,1,0:T(8,128)(2,1)S(1)}, u32[]{:S(2)}, u32[]{:S(2)}) async-start(bf16[8,32,2048]{2,1,0:T(8,128)(2,1)} %bitcast.5), calls=%async_computation | async-start | bytes 2097152 | tf_op jit(solution)/shard_map/all_to_all | solution.py:312
  39.6 21.2 %weight_grads.1 = (f32[4096,1792]{1,0:T(8,128)}, f32[1792,4096]{1,0:T(8,128)}) custom-call(bf16[256,4096]{1,0:T(8,128)(2,1)} %get-tuple-element.11.xg, bf16[256,4096]{1,0:T(8,128)(2,1)} %get-tuple-element.12.dyg, bf16[256,1792]{1,0:T(8,128)(2,1)} %get-tuple-element.13.z, bf16[256,1792]{1,0:T(8,128)(2,1)} %get-tuple-element.14.dz), custom_call_target="tpu_custom_call" | custom-call | flops 7516192768 | bytes 58720256 | tf_op jit(solution)/shard_map/weight_grads/pallas_call | solution.py:314
  60.9 0.0 all-to-all-done
  60.9 0.2 convert_element_type.4
  61.1 0.1 fusion.2
  61.2 0.7 %pad_maximum_fusion = bf16[32,4096]{1,0:T(8,128)(2,1)} fusion(bf16[32,2048]{1,0:T(8,128)(2,1)S(1)} %get-tuple-element.18, bf16[32,2048]{1,0:T(8,128)(2,1)S(1)} %get-tuple-element.17), kind=kLoop, calls=%fused_computation.8 | loop fusion | flops 524288 | bytes 524288 | tf_op jit(solution)/shard_map/concatenate | solution.py:333
Async XLA Ops:
  35.9 25.0 %all-to-all-start = ((bf16[8,32,2048]{2,1,0:T(8,128)(2,1)}), bf16[8,32,2048]{2,1,0:T(8,128)(2,1)S(1)}, u32[]{:S(2)}, u32[]{:S(2)}) async-start(bf16[8,32,2048]{2,1,0:T(8,128)(2,1)} %bitcast.5), calls=%async_computation | async-start | bytes 2097152 | tf_op jit(solution)/shard_map/all_to_all | solution.py:312
where the time goes:
time: 62.1 us; the launch traced here: 62 us
  Pallas kernels  56.5 us (91%)
  starting transfers between devices  3.73 us (6%)
  other arithmetic  1.06 us (2%)
  between operations  0.67 us (1%)
    pallas_call x1, Pallas kernels, body(): pl.pallas_call(functools.partial(_forward_kernel, ntp), name='gather_forw...  35.3 us
    pallas_call x1, Pallas kernels, body(): pl.pallas_call(_weight_grad_kernel, name='weight_grads', out_shape=[sds((...  21.2 us
    all_to_all x1, starting transfers between devices, body(): r = lax.all_to_all(r.reshape(ntp, rows, half), 'tp', 0, 0, tiled=True)  3.73 us
  transfers between devices with their start and end apart: 1, of which 0 were waited for; matrix products, arithmetic and copies ran while one was open for 0% of the time, Pallas kernels for 34%

commit v1 on v0

--- a/solution.py
+++ b/solution.py
@@ -13,7 +13,7 @@
 F32 = jnp.float32
 BF16 = jnp.bfloat16
 NP = 4
-NW = 16
+NW = 8
 TILE = 896
 XC = (2, 2, 2, 2)
 YC = (2, 2, 2, 1, 1)
@@ -222,7 +222,7 @@
     cy = [pltpu.make_async_copy(dyg.at[:, pl.ds(q * hc, hc)], dya.at[:, pl.ds(q * hc, hc)], isem.at[1 + q]) for q in range(nq)]
     cx = pltpu.make_async_copy(xg, xa, isem.at[1 + nq])
     cd = pltpu.make_async_copy(dz, dza, isem.at[2 + nq])
-    for cp in [cz] + cy + [cd, cx]:
+    for cp in [cz] + cy:
         cp.start()
     cz.wait()
 
@@ -236,6 +236,9 @@
 
     for q in range(nq):
         cy[q].wait()
+        if q == 2:
+            cd.start()
+            cx.start()
         b2[0, :, pl.ds(q * hc, hc)] = lax.dot_general(za[:, :t2], dya[:, pl.ds(q * hc, hc)], TN, preferred_element_type=F32)
     out2(0).start()
 
@@ -310,7 +313,7 @@
         )(x, dy, w1, w2)
 
         r = lax.all_to_all(r.reshape(ntp, rows, half), 'tp', 0, 0, tiled=True)
-        t1, t2 = 512, 256
+        t1, t2 = 256, 128
         dw1, dw2 = pl.pallas_call(
             _weight_grad_kernel,
             name='weight_grads',
@@ -322,15 +325,15 @@
                 pltpu.VMEM((t, h), BF16),
                 pltpu.VMEM((t, f), BF16),
                 pltpu.VMEM((t, f), BF16),
-                pltpu.VMEM((4, t1, f), F32),
-                pltpu.VMEM((4, t2, h), F32),
-                dma((7,)), dma((4,)), dma((4,)),
+                pltpu.VMEM((8, t1, f), F32),
+                pltpu.VMEM((8, t2, h), F32),
+                dma((7,)), dma((8,)), dma((8,)),
             ],
             compiler_params=pltpu.CompilerParams(vmem_limit_bytes=VMEM_LIMIT),
             cost_estimate=pl.CostEstimate(flops=4 * t * h * f, bytes_accessed=8 * h * f, transcendentals=0),
         )(xg, dyg, z, dz)
-        r = r.astype(F32)
-        dx = jnp.concatenate([sum(r[2 * i + k] for i in range(nchip)) for k in range(2)], axis=1).astype(BF16)
+        r = r.reshape(nchip, 2, rows, half)
+        dx = jnp.sum(jnp.concatenate([r[:, 0], r[:, 1]], axis=2).astype(F32), axis=0).astype(BF16)
         return dx, dw1, dw2
 
     return jax.shard_map(

time: 62.1 us -> 61.4 us (0.989)
    reduce_sum x0 -> x1, other arithmetic: none -> 0.85 us  [body(): jnp.sum(jnp.concatenate([r[:, 0], r[:, 1]], axis=2).astype(F32), axis=0)]
    concatenate x1 -> x0, other arithmetic: 0.72 us -> none  [body(): jnp.concatenate([sum((r[2 * i + k] for i in range(nchip))) for k in range...]
where the time goes in v1:
time: 61.4 us; the launch traced here: 61.2 us
  Pallas kernels  55.9 us (91%)
  starting transfers between devices  3.73 us (6%)
  other arithmetic  0.85 us (1%)
  between operations  0.66 us (1%)
    pallas_call x1, Pallas kernels, body(): pl.pallas_call(functools.partial(_forward_kernel, ntp), name='gather_forw...  34.9 us
    pallas_call x1, Pallas kernels, body(): pl.pallas_call(_weight_grad_kernel, name='weight_grads', out_shape=[sds((...  21 us
    all_to_all x1, starting transfers between devices, body(): r = lax.all_to_all(r.reshape(ntp, rows, half), 'tp', 0, 0, tiled=True)  3.73 us
  transfers between devices with their start and end apart: 1, of which 0 were waited for; matrix products, arithmetic and copies ran while one was open for 0% of the time, Pallas kernels for 34%

profile of v1, /device:TPU:113, one launch (start us, length us, event | category | flops | bytes accessed | tf_op | source)
XLA Modules:
  0.0 61.2 jit_solution(7534619157871970679)
XLA Ops:
  0.6 34.9 %gather_forward.1 = (bf16[256,4096]{1,0:T(8,128)(2,1)}, bf16[256,4096]{1,0:T(8,128)(2,1)}, bf16[256,1792]{1,0:T(8,128)(2,1)}, bf16[256,1792]{1,0:T(8,128)(2,1)}, bf16[256,2048]{1,0:T(8,128)(2,1)}) custom-call(bf16[32,4096]{1,0:T(8,128)(2,1)} %x.1, bf16[32,4096]{1,0:T(8,128)(2,1)} %dy.1, bf16[4096,1792]{1,0:T(8,128)(2,1)} %w1.1, bf16[1792,4096]{1,0:T(8,128)(2,1)} %w2.1), custom_call_target="tpu_custom_call" | custom-call | flops 11274289152 | bytes 29360128 | tf_op jit(solution)/shard_map/gather_forward/pallas_call | solution.py:287
  35.6 3.7 %all-to-all-start = ((bf16[8,32,2048]{2,1,0:T(8,128)(2,1)}), bf16[8,32,2048]{2,1,0:T(8,128)(2,1)S(1)}, u32[]{:S(2)}, u32[]{:S(2)}) async-start(bf16[8,32,2048]{2,1,0:T(8,128)(2,1)} %bitcast.9), calls=%async_computation | async-start | bytes 2097152 | tf_op jit(solution)/shard_map/all_to_all | solution.py:315
  39.3 21.0 %weight_grads.1 = (f32[4096,1792]{1,0:T(8,128)}, f32[1792,4096]{1,0:T(8,128)}) custom-call(bf16[256,4096]{1,0:T(8,128)(2,1)} %get-tuple-element.11.xg, bf16[256,4096]{1,0:T(8,128)(2,1)} %get-tuple-element.12.dyg, bf16[256,1792]{1,0:T(8,128)(2,1)} %get-tuple-element.13.z, bf16[256,1792]{1,0:T(8,128)(2,1)} %get-tuple-element.14.dz), custom_call_target="tpu_custom_call" | custom-call | flops 7516192768 | bytes 58720256 | tf_op jit(solution)/shard_map/weight_grads/pallas_call | solution.py:317
  60.3 0.0 all-to-all-done
  60.3 0.1 slice_bitcast_fusion.1
  60.4 0.8 %maximum_reduce_fusion = bf16[32,4096]{1,0:T(8,128)(2,1)} fusion(bf16[4,32,2048]{2,1,0:T(8,128)(2,1)S(1)} %get-tuple-element.18, bf16[4,32,2048]{2,1,0:T(8,128)(2,1)S(1)} %get-tuple-element.17), kind=kLoop, calls=%fused_computation | loop fusion | flops 2490368 | bytes 1310720 | tf_op jit(solution)/shard_map/reduce_sum | solution.py:336
Async XLA Ops:
  35.6 24.7 %all-to-all-start = ((bf16[8,32,2048]{2,1,0:T(8,128)(2,1)}), bf16[8,32,2048]{2,1,0:T(8,128)(2,1)S(1)}, u32[]{:S(2)}, u32[]{:S(2)}) async-start(bf16[8,32,2048]{2,1,0:T(8,128)(2,1)} %bitcast.9), calls=%async_computation | async-start | bytes 2097152 | tf_op jit(solution)/shard_map/all_to_all | solution.py:315

commit v2 on v1

--- a/solution.py
+++ b/solution.py
@@ -75,7 +75,8 @@
     for q, (src, buf, cols) in enumerate(chunks):
         wr, wb = (w1.at[cols, :], w1v.at[cols, :]) if q < nx else (w2.at[:, cols], w2v.at[:, cols])
         cp = pltpu.make_async_copy(wr, wb, wsem.at[q])
-        cp.start()
+        if q < nx:
+            cp.start()
         wcp.append(cp)
 
     barrier = pltpu.get_barrier_semaphore()
@@ -184,6 +185,8 @@
         if s == GIVE:
             for q in range(nx):
                 wcp[q].wait()
+            for q in range(nx, nq):
+                wcp[q].start()
         if GIVE <= s < nq:
             for i in range(given, NW * (s - GIVE + 1) // (nq - GIVE)):
                 begin(weights(i))

time: 61.4 us -> 61.4 us (level)
  no operation moved by 1% of the time
where the time goes in v2:
time: 61.4 us; the launch traced here: 61.2 us
  Pallas kernels  55.9 us (91%)
  starting transfers between devices  3.73 us (6%)
  other arithmetic  0.85 us (1%)
  between operations  0.66 us (1%)
    pallas_call x1, Pallas kernels, body(): pl.pallas_call(functools.partial(_forward_kernel, ntp), name='gather_forw...  34.9 us
    pallas_call x1, Pallas kernels, body(): pl.pallas_call(_weight_grad_kernel, name='weight_grads', out_shape=[sds((...  21 us
    all_to_all x1, starting transfers between devices, body(): r = lax.all_to_all(r.reshape(ntp, rows, half), 'tp', 0, 0, tiled=True)  3.73 us
  transfers between devices with their start and end apart: 1, of which 0 were waited for; matrix products, arithmetic and copies ran while one was open for 0% of the time, Pallas kernels for 34%

profile of v2, /device:TPU:113, one launch (start us, length us, event | category | flops | bytes accessed | tf_op | source)
XLA Modules:
  0.0 61.2 jit_solution(13234288514879691824)
XLA Ops:
  0.6 34.9 %gather_forward.1 = (bf16[256,4096]{1,0:T(8,128)(2,1)}, bf16[256,4096]{1,0:T(8,128)(2,1)}, bf16[256,1792]{1,0:T(8,128)(2,1)}, bf16[256,1792]{1,0:T(8,128)(2,1)}, bf16[256,2048]{1,0:T(8,128)(2,1)}) custom-call(bf16[32,4096]{1,0:T(8,128)(2,1)} %x.1, bf16[32,4096]{1,0:T(8,128)(2,1)} %dy.1, bf16[4096,1792]{1,0:T(8,128)(2,1)} %w1.1, bf16[1792,4096]{1,0:T(8,128)(2,1)} %w2.1), custom_call_target="tpu_custom_call" | custom-call | flops 11274289152 | bytes 29360128 | tf_op jit(solution)/shard_map/gather_forward/pallas_call | solution.py:290
  35.6 3.7 %all-to-all-start = ((bf16[8,32,2048]{2,1,0:T(8,128)(2,1)}), bf16[8,32,2048]{2,1,0:T(8,128)(2,1)S(1)}, u32[]{:S(2)}, u32[]{:S(2)}) async-start(bf16[8,32,2048]{2,1,0:T(8,128)(2,1)} %bitcast.9), calls=%async_computation | async-start | bytes 2097152 | tf_op jit(solution)/shard_map/all_to_all | solution.py:318
  39.3 21.0 %weight_grads.1 = (f32[4096,1792]{1,0:T(8,128)}, f32[1792,4096]{1,0:T(8,128)}) custom-call(bf16[256,4096]{1,0:T(8,128)(2,1)} %get-tuple-element.11.xg, bf16[256,4096]{1,0:T(8,128)(2,1)} %get-tuple-element.12.dyg, bf16[256,1792]{1,0:T(8,128)(2,1)} %get-tuple-element.13.z, bf16[256,1792]{1,0:T(8,128)(2,1)} %get-tuple-element.14.dz), custom_call_target="tpu_custom_call" | custom-call | flops 7516192768 | bytes 58720256 | tf_op jit(solution)/shard_map/weight_grads/pallas_call | solution.py:320
  60.3 0.0 all-to-all-done
  60.3 0.1 slice_bitcast_fusion.1
  60.4 0.8 %maximum_reduce_fusion = bf16[32,4096]{1,0:T(8,128)(2,1)} fusion(bf16[4,32,2048]{2,1,0:T(8,128)(2,1)S(1)} %get-tuple-element.18, bf16[4,32,2048]{2,1,0:T(8,128)(2,1)S(1)} %get-tuple-element.17), kind=kLoop, calls=%fused_computation | loop fusion | flops 2490368 | bytes 1310720 | tf_op jit(solution)/shard_map/reduce_sum | solution.py:339
Async XLA Ops:
  35.6 24.7 %all-to-all-start = ((bf16[8,32,2048]{2,1,0:T(8,128)(2,1)}), bf16[8,32,2048]{2,1,0:T(8,128)(2,1)S(1)}, u32[]{:S(2)}, u32[]{:S(2)}) async-start(bf16[8,32,2048]{2,1,0:T(8,128)(2,1)} %bitcast.9), calls=%async_computation | async-start | bytes 2097152 | tf_op jit(solution)/shard_map/all_to_all | solution.py:318
